TPU v7x, 32 devices: a whole 2x2x4 slice. The times are simulated.
32 devices in a mesh: rows: 4 (over z), cols: 8 (over y, x, core).
Axes of the slice: x: 2, y: 2, z: 4, core: 2. Of those that a mesh axis runs over, the one named last changes fastest.
Arguments:
- features: bfloat16 [65536, 440], P(('rows', 'cols')), may hold values from -12 to 12
- residual: float32 [65536, 147], P(('rows', 'cols')), may hold values from -6 to 6
- coeffs: float32 [65536, 147], P(('rows', 'cols')), may hold values from -3 to 3
- block_inverse: float32 [2, 2048, 2048], P(None, ('rows', 'cols')), may hold values from -0.0234375 to 0.0234375
- block_index: int32 [2, 2048], P(None, 'cols'), may hold values from 0 to 2047, as said below
- owners: int32 [2], replicated, may hold values from 0 to 3
Outputs:
- new_coeffs: float32 [65536, 147], P(('rows', 'cols'))
- new_residual: float32 [65536, 147], P(('rows', 'cols'))
Inputs may be any that keep to these rules, and one draw needn't show every extreme that they name: `block_index`: for each step and each aligned run of 256 positions, the indices are distinct.
All inputs are finite; a program needn't handle non-finite values.
Results may differ from a plain program's by a relative error of at most 0.0028.
Values may be sent and summed in bfloat16 or wider, within the bound.
No kernel may reach another device: no remote copies, remote signals or barrier semaphores. Data moves between devices by JAX's collectives and lax.ppermute only.
A program may use at most 64 MiB of HBM per device.

v0:
```python
import jax
import jax.numpy as jnp
from jax import lax
from jax.sharding import PartitionSpec as P

penalty = 0.5


def from_root(value, axis, source):
    kept = jnp.where(lax.axis_index(axis) == source, value, 0).astype(value.dtype)
    return lax.psum(kept, axis)


def per_device(features, residual, coeffs, block_inverse, block_index, owners):
    frame_count = features.shape[0]
    feature_width = features.shape[1]
    per_col = block_index.shape[1]
    row_block = min(512, frame_count)
    exponent = -1.0 / feature_width
    my_row = lax.axis_index("rows")
    my_col = lax.axis_index("cols")
    squares = jnp.sum(jnp.square(features.astype(jnp.float32)), axis=1)
    feature_blocks = features.reshape(frame_count // row_block, row_block, feature_width)
    norm_blocks = squares.reshape(frame_count // row_block, row_block)
    for step_id in range(block_index.shape[0]):
        chosen_rows = block_index[step_id]
        owner_row = owners[step_id]
        mine_feat = jnp.take(features, chosen_rows, axis=0)
        mine_res = jnp.take(residual, chosen_rows, axis=0)
        row_piece = from_root(mine_feat, "rows", owner_row)
        chosen = lax.all_gather(row_piece, "cols", axis=0, tiled=True)
        res_piece = from_root(mine_res, "rows", owner_row)
        picked_res = lax.all_gather(res_piece, "cols", axis=0, tiled=True)
        my_update = jnp.dot(
            block_inverse[step_id],
            picked_res,
            precision=lax.Precision.HIGHEST,
            preferred_element_type=jnp.float32,
        ).astype(jnp.bfloat16)
        update = lax.all_gather(my_update, ("rows", "cols"), axis=0, tiled=True)
        chosen_norms = jnp.sum(jnp.square(chosen.astype(jnp.float32)), axis=1)

        def kernel_rows(operands):
            block_rows, block_norms = operands
            inner = lax.dot_general(
                block_rows, chosen, (((1,), (1,)), ((), ())), preferred_element_type=jnp.float32
            )
            distance = block_norms[:, None] + chosen_norms[None, :] - 2.0 * inner
            kernel = jnp.exp(distance * exponent).astype(jnp.bfloat16)
            return jnp.dot(kernel, update, preferred_element_type=jnp.float32)

        change = lax.map(kernel_rows, (feature_blocks, norm_blocks)).reshape(frame_count, -1)
        residual = residual - change
        is_owner = jnp.where(my_row == owner_row, 1.0, 0.0).astype(jnp.float32)
        mine_update = (
            lax.dynamic_slice_in_dim(update, my_col * per_col, per_col, 0).astype(jnp.float32)
            * is_owner
        )
        residual = residual.at[chosen_rows].add(-penalty * mine_update)
        coeffs = coeffs.at[chosen_rows].add(mine_update)
    return (coeffs, residual)


def solution(mesh):
    in_specs = (
        P(("rows", "cols"), None),
        P(("rows", "cols"), None),
        P(("rows", "cols"), None),
        P(None, ("rows", "cols"), None),
        P(None, "cols"),
        P(),
    )
    out_specs = (P(("rows", "cols"), None), P(("rows", "cols"), None))
    return jax.shard_map(
        per_device, mesh=mesh, in_specs=in_specs, out_specs=out_specs, check_vma=False
    )
```

profile of v0, /device:TPU:0, one launch (start us, length us, event | category | flops | bytes accessed | tf_op | source)
XLA Modules:
  0.0 380.8 jit_solution(9416683391688885127)
XLA Ops:
  13.6 3.8 %copy.18 = bf16[2048,440]{1,0:T(8,128)(2,1)} copy(bf16[2048,440]{0,1:T(8,128)(2,1)} %param.14) | data formatting | bytes 3604480 | tf_op args[0]
  17.5 3.1 gather_fusion.1
  20.6 3.2 gather_fusion.3
  25.6 26.5 %all-reduce.5.cloned.1.call-done = f32[256,147]{1,0:T(8,128)} async-done(((f32[256,147]{1,0:T(8,128)}), f32[256,147]{1,0:T(8,128)}) %all-reduce.5.cloned.1.call-update) | async-done | bytes 150544 | tf_op jit(solution)/shard_map/psum | solution.py:11
  52.1 41.4 %all-reduce.9.cloned.1.call-done = (bf16[256,440]{1,0:T(8,128)(2,1)}, bf16[256,440]{1,0:T(8,128)(2,1)}) async-done(((bf16[256,440]{1,0:T(8,128)(2,1)}, bf16[256,440]{1,0:T(8,128)(2,1)}), (bf16[256,440]{1,0:T(8,128)(2,1)}, bf16[256,440]{1,0:T(8,128)(2,1)})) %all-reduce.9.cloned.1.call-update) | async-done | bytes 450576 | tf_op jit(solution)/shard_map/psum | solution.py:11
  94.0 29.0 %all-gather.5.cloned.1.call-done = f32[2048,147]{1,0:T(8,128)} async-done(((f32[256,147]{1,0:T(8,128)}), f32[2048,147]{1,0:T(8,128)}) %all-gather.5.cloned.1.call-update) | async-done | bytes 1204240 | tf_op jit(solution)/shard_map/all_gather | solution.py:33
  123.1 2.9 fusion.18
  126.0 46.2 %all_gather.19 = bf16[2048,147]{1,0:T(8,128)(2,1)} all-gather(bf16[64,147]{1,0:T(8,128)(2,1)S(1)} %fusion.18), channel_id=1, replica_groups=mesh['rows'=4,'cols'=8] {'rows','cols'}, dimensions={0}, use_global_device_ids=true | all-gather | bytes 620928 | tf_op jit(solution)/shard_map/all_gather | solution.py:40
  172.2 2.3 multiply_reduce_fusion.1
  174.6 14.1 %while.20 = (s32[]{:T(128)}, f32[4,512,147]{1,2,0:T(8,128)S(1)}, f32[4,512]{1,0:T(4,128)S(1)}, f32[2048]{0:T(1024)S(1)}, bf16[4,512,440]{2,1,0:T(8,128)(2,1)}, /...) while((s32[]{:T(128)}, f32[4,512,147]{1,2,0:T(8,128)S(1)}, f32[4,512]{1,0:T(4,128)S(1)}, ...), condition=%wide.region_6.9_spmd, body=%wide.region_5.8_spmd.sunk | while | flops 1236271104 | bytes 3996761 | solution.py:52
  174.6 3.5 fusion.59
  178.2 3.5 fusion.59
  181.7 3.5 fusion.59
  185.2 3.5 fusion.59
  190.5 2.5 bitcast_subtract_fusion.1
  193.0 3.1 scatter_custom_fusion.1
  200.4 31.0 %all-reduce.7.cloned.1.call-done = f32[256,147]{1,0:T(8,128)} async-done(((f32[256,147]{1,0:T(8,128)}), f32[256,147]{1,0:T(8,128)}) %all-reduce.7.cloned.1.call-update) | async-done | bytes 150544 | tf_op jit(solution)/shard_map/psum | solution.py:11
  233.3 5.2 %scatter_custom_fusion = f32[2048,147]{1,0:T(8,128)} fusion(f32[2048,147]{1,0:T(8,128)} %copy.17, s32[256]{0:T(256)S(1)} %bitcast.79, f32[]{:T(128)S(6)} %select_n.78, bf16[2048,147]{1,0:T(8,128)(2,1)} %get-tuple-element.271, s32[]{:T(128)S(6)} %select_n.77, s32[]{:T(128)} %constant.43.clone.1), kind=kCustom, calls=%fused_computation.50 | custom fusion | flops 112896 | bytes 1335816 | tf_op jit(solution)/shard_map/scatter-add | solution.py:60
  238.5 22.4 %all-gather.11.cloned.1.call-done = bf16[2048,440]{1,0:T(8,128)(2,1)} async-done(((bf16[256,440]{1,0:T(8,128)(2,1)}), bf16[2048,440]{1,0:T(8,128)(2,1)}) %all-gather.11.cloned.1.call-update) | async-done | bytes 1802256 | tf_op jit(solution)/shard_map/all_gather | solution.py:31
  260.9 2.1 multiply_reduce_fusion
  263.0 27.6 %all-gather.9.cloned.1.call-done = f32[2048,147]{1,0:T(8,128)} async-done(((f32[256,147]{1,0:T(8,128)}), f32[2048,147]{1,0:T(8,128)}) %all-gather.9.cloned.1.call-update) | async-done | bytes 1204240 | tf_op jit(solution)/shard_map/all_gather | solution.py:33
  290.6 2.9 fusion.19
  293.5 46.1 %all_gather.22 = bf16[2048,147]{1,0:T(8,128)(2,1)} all-gather(bf16[64,147]{1,0:T(8,128)(2,1)S(1)} %fusion.19), channel_id=1, replica_groups=mesh['rows'=4,'cols'=8] {'rows','cols'}, dimensions={0}, use_global_device_ids=true | all-gather | bytes 620928 | tf_op jit(solution)/shard_map/all_gather | solution.py:40
  339.7 16.6 %while.21 = (s32[]{:T(128)}, f32[4,512,147]{1,2,0:T(8,128)S(1)}, f32[4,512]{1,0:T(4,128)S(1)}, f32[2048]{0:T(1024)S(1)}, bf16[4,512,440]{2,1,0:T(8,128)(2,1)}, /...) while((s32[]{:T(128)}, f32[4,512,147]{1,2,0:T(8,128)S(1)}, f32[4,512]{1,0:T(4,128)S(1)}, ...), condition=%wide.region_13.16_spmd, body=%wide.region_12.15_spmd.sunk | while | flops 1236271104 | bytes 3996761 | solution.py:52
  339.7 4.1 %fusion.63 = f32[4,512,147]{1,2,0:T(8,128)S(1)} fusion(f32[4,512,147]{1,2,0:T(8,128)S(1)} %get-tuple-element.241, s32[]{:T(128)} %get-tuple-element.240, bf16[2048,147]{1,0:T(8,128)(2,1)} %get-tuple-element.254, bf16[2048,440]{1,0:T(8,128)(2,1)} %get-tuple-element.253, f32[2048]{0:T(1024)S(1)} %get-tuple-element.251, f32[512]{0:T(512)S(1)} %bitcast.71, ...), kind=kOutput, calls=%fused_computation.19.clone.1 | convolution fusion | flops 1236271104 | bytes 3992576 | tf_op jit(solution)/shard_map/while/body/eval_jaxpr/dot_general | solution.py:50
  343.9 4.1 %fusion.63 = f32[4,512,147]{1,2,0:T(8,128)S(1)} fusion(f32[4,512,147]{1,2,0:T(8,128)S(1)} %get-tuple-element.241, s32[]{:T(128)} %get-tuple-element.240, bf16[2048,147]{1,0:T(8,128)(2,1)} %get-tuple-element.254, bf16[2048,440]{1,0:T(8,128)(2,1)} %get-tuple-element.253, f32[2048]{0:T(1024)S(1)} %get-tuple-element.251, f32[512]{0:T(512)S(1)} %bitcast.71, ...), kind=kOutput, calls=%fused_computation.19.clone.1 | convolution fusion | flops 1236271104 | bytes 3992576 | tf_op jit(solution)/shard_map/while/body/eval_jaxpr/dot_general | solution.py:50
  348.1 4.1 %fusion.63 = f32[4,512,147]{1,2,0:T(8,128)S(1)} fusion(f32[4,512,147]{1,2,0:T(8,128)S(1)} %get-tuple-element.241, s32[]{:T(128)} %get-tuple-element.240, bf16[2048,147]{1,0:T(8,128)(2,1)} %get-tuple-element.254, bf16[2048,440]{1,0:T(8,128)(2,1)} %get-tuple-element.253, f32[2048]{0:T(1024)S(1)} %get-tuple-element.251, f32[512]{0:T(512)S(1)} %bitcast.71, ...), kind=kOutput, calls=%fused_computation.19.clone.1 | convolution fusion | flops 1236271104 | bytes 3992576 | tf_op jit(solution)/shard_map/while/body/eval_jaxpr/dot_general | solution.py:50
  352.2 4.1 %fusion.63 = f32[4,512,147]{1,2,0:T(8,128)S(1)} fusion(f32[4,512,147]{1,2,0:T(8,128)S(1)} %get-tuple-element.241, s32[]{:T(128)} %get-tuple-element.240, bf16[2048,147]{1,0:T(8,128)(2,1)} %get-tuple-element.254, bf16[2048,440]{1,0:T(8,128)(2,1)} %get-tuple-element.253, f32[2048]{0:T(1024)S(1)} %get-tuple-element.251, f32[512]{0:T(512)S(1)} %bitcast.71, ...), kind=kOutput, calls=%fused_computation.19.clone.1 | convolution fusion | flops 1236271104 | bytes 3992576 | tf_op jit(solution)/shard_map/while/body/eval_jaxpr/dot_general | solution.py:50
  358.1 3.2 bitcast_subtract_fusion
  361.3 5.1 %scatter_custom_fusion.3 = f32[2048,147]{1,0:T(8,128)} fusion(f32[2048,147]{1,0:T(8,128)} %bitcast_subtract_fusion, s32[256]{0:T(256)S(1)} %bitcast.76, f32[]{:T(128)S(6)} %select_n.84, f32[]{:T(128)} %constant.72.clone.1, bf16[2048,147]{1,0:T(8,128)(2,1)} %get-tuple-element.272, s32[]{:T(128)S(6)} %select_n.77, s32[]{:T(128)} %constant.43.clone.1), kind=kCustom, calls=%fused_computation.43 | custom fusion | flops 150528 | bytes 1336328 | tf_op jit(solution)/shard_map/scatter-add | solution.py:59
  366.4 2.8 copy.25
  369.2 3.1 scatter_custom_fusion.2
  (62 shorter events, 18.9 us)
Async XLA Ops:
  7.2 44.9 %all-reduce.5.cloned.1.call-start = ((), (), s32[]{:S(2)}) async-start(), calls=%async_computation | async-start | bytes 524288 | tf_op jit(solution)/shard_map/psum | solution.py:11
  11.1 6.4 %copy-start = (f32[2048,147]{1,0:T(8,128)}, f32[2048,147]{1,0:T(8,128)S(1)}, u32[]{:S(2)}) copy-start(f32[2048,147]{1,0:T(8,128)S(1)} %copy.16) | copy-start | bytes 3612676
  13.6 80.0 %all-reduce.9.cloned.1.call-start = ((), (), s32[]{:S(2)}) async-start(), calls=%async_computation.6 | async-start | bytes 1048576 | tf_op jit(solution)/shard_map/psum | solution.py:11
  20.5 73.1 %copy-start.2 = (bf16[2048,440]{0,1:T(8,128)(2,1)S(1)}, bf16[2048,440]{0,1:T(8,128)(2,1)}, u32[]{:S(2)}) copy-start(bf16[2048,440]{0,1:T(8,128)(2,1)} %param.14) | copy-start | bytes 5406724
  23.8 70.2 %copy-start.7 = (s32[2,256]{1,0:T(2,128)S(1)}, s32[2,256]{1,0:T(2,128)}, u32[]{:S(2)}) copy-start(s32[2,256]{1,0:T(2,128)} %param.18) | copy-start | bytes 6148
  23.8 99.3 %copy-start.5 = (f32[2,64,2048]{2,1,0:T(8,128)S(1)}, f32[2,64,2048]{2,1,0:T(8,128)}, u32[]{:S(2)}) copy-start(f32[2,64,2048]{2,1,0:T(8,128)} %param.17) | copy-start | bytes 3145732
  25.5 97.5 %all-gather.5.cloned.1.call-start = ((), (), s32[]{:S(2)}) async-start(), calls=%async_computation.1 | async-start | bytes 2359296 | tf_op jit(solution)/shard_map/all_gather | solution.py:33
  52.1 120.1 %all-gather.7.cloned.1.call-start = ((), (), s32[]{:S(2)}) async-start(), calls=%async_computation.2 | async-start | bytes 2359296 | tf_op jit(solution)/shard_map/all_gather | solution.py:31
  93.6 137.9 %all-reduce.7.cloned.1.call-start = ((), (), s32[]{:S(2)}) async-start(), calls=%async_computation.3 | async-start | bytes 524288 | tf_op jit(solution)/shard_map/psum | solution.py:11
  172.2 2.4 copy-start.3
  196.1 35.3 %copy-start.4 = (f32[2048,147]{0,1:T(8,128)S(1)}, f32[2048,147]{0,1:T(8,128)}, u32[]{:S(2)}) copy-start(f32[2048,147]{0,1:T(8,128)} %param.16) | copy-start | bytes 3612676
  199.6 61.3 %all-gather.11.cloned.1.call-start = ((), (), s32[]{:S(2)}) async-start(), calls=%async_computation.5 | async-start | bytes 2359296 | tf_op jit(solution)/shard_map/all_gather | solution.py:31
  200.2 90.4 %all-gather.9.cloned.1.call-start = ((), (), s32[]{:S(2)}) async-start(), calls=%async_computation.4 | async-start | bytes 2359296 | tf_op jit(solution)/shard_map/all_gather | solution.py:33
  233.3 57.3 %copy-start.6 = (f32[2,64,2048]{2,1,0:T(8,128)S(1)}, f32[2,64,2048]{2,1,0:T(8,128)}, u32[]{:S(2)}) copy-start(f32[2,64,2048]{2,1,0:T(8,128)} %param.17) | copy-start | bytes 3145732
  366.4 2.8 copy-start.1
Sparse Core Ops, SparseCore 0:
  13.7 38.3 all-reduce.4
  55.0 38.4 all-reduce.8
  95.4 27.5 all-gather.4
  124.8 31.5 all-gather.6
  199.7 31.6 all-reduce.6
  233.2 27.6 all-gather.10
  262.8 27.7 all-gather.8
where the time goes:
time: 382 us; the launch traced here: 381 us
  waiting for transfers between devices  179 us (47%)
  blocking collectives  92.3 us (24%)
  matrix products  36.3 us (10%)
  other arithmetic  30.5 us (8%)
  local copies, waits for them, and re-layouts  26.8 us (7%)
  between operations  15.7 us (4%)
    psum x3, waiting for transfers between devices, from_root(): return lax.psum(kept, axis)  98.9 us
    all_gather x2, blocking collectives, per_device(): update = lax.all_gather(my_update, ('rows', 'cols'), axis=0, tiled=True)  92.3 us
    all_gather x2, waiting for transfers between devices, per_device(): picked_res = lax.all_gather(res_piece, 'cols', axis=0, tiled=True)  56.6 us
    dot_general x8, matrix products, kernel_rows(): return jnp.dot(kernel, update, preferred_element_type=jnp.float32)  30.5 us
    all_gather x2, waiting for transfers between devices, per_device(): chosen = lax.all_gather(row_piece, 'cols', axis=0, tiled=True)  22.4 us
    unnamed x21, local copies, waits for them, and re-layouts  11.9 us
    scatter-add x2, other arithmetic, per_device(): coeffs = coeffs.at[chosen_rows].add(mine_update)  8.29 us
    scatter-add x2, other arithmetic, per_device(): residual = residual.at[chosen_rows].add(-penalty * mine_update)  8.22 us
  transfers between devices with their start and end apart: 7, of which 6 were waited for; matrix products, arithmetic and copies ran while one was open for 6% of the time, Pallas kernels for 0%

commit v1 on v0

--- a/solution.py
+++ b/solution.py
@@ -4,6 +4,18 @@
 from jax.sharding import PartitionSpec as P
 
 penalty = 0.5
+
+
+def gather_by_bits(shard, axis, dim):
+    ways, here = (lax.axis_size(axis), lax.axis_index(axis))
+    grown, reach = (shard, 1)
+    while reach < ways:
+        theirs = lax.ppermute(grown, axis, [(d, d ^ reach) for d in range(ways)])
+        mine_first = jnp.concatenate([grown, theirs], axis=dim)
+        theirs_first = jnp.concatenate([theirs, grown], axis=dim)
+        grown = jnp.where(here & reach == 0, mine_first, theirs_first)
+        reach = 2 * reach
+    return grown
 
 
 def from_root(value, axis, source):
@@ -37,7 +49,7 @@
             precision=lax.Precision.HIGHEST,
             preferred_element_type=jnp.float32,
         ).astype(jnp.bfloat16)
-        update = lax.all_gather(my_update, ("rows", "cols"), axis=0, tiled=True)
+        update = gather_by_bits(my_update, ("rows", "cols"), 0)
         chosen_norms = jnp.sum(jnp.square(chosen.astype(jnp.float32)), axis=1)
 
         def kernel_rows(operands):

time: 382 us -> 347 us (0.908)
  blocking collectives: 92.3 us -> 0 us
  waiting for transfers between devices: 179 us -> 217 us
  starting transfers between devices: 0.46 us -> 17.7 us
    all_gather x2 -> x0, blocking collectives: 92.3 us -> none  [per_device(): update = lax.all_gather(my_update, ('rows', 'cols'), axis=0, tiled=True)]
    ppermute x0 -> x10, waiting for transfers between devices: none -> 54.1 us  [gather_by_bits(): theirs = lax.ppermute(grown, axis, [(d, d ^ reach) for d in range(ways)])]
    all_gather x2, waiting for transfers between devices: 22.4 us -> 0.01 us  [per_device(): chosen = lax.all_gather(row_piece, 'cols', axis=0, tiled=True)]
    ppermute x0 -> x10, starting transfers between devices: none -> 17.2 us  [gather_by_bits(): theirs = lax.ppermute(grown, axis, [(d, d ^ reach) for d in range(ways)])]
    psum x3, waiting for transfers between devices: 98.9 us -> 104 us  [from_root(): return lax.psum(kept, axis)]
    unnamed x21 -> x19, local copies, waits for them, and re-layouts: 11.9 us -> 12.9 us
  transfers between devices with their start and end apart: 7 -> 17, of which waited for: 6 -> 15; matrix products, arithmetic and copies ran while one was open for 6% -> 8% of each run, Pallas kernels for 0% -> 0%
where the time goes in v1:
time: 347 us
  waiting for transfers between devices  217 us (63%)
  matrix products  36.3 us (10%)
  other arithmetic  32.6 us (9%)
  local copies, waits for them, and re-layouts  27.1 us (8%)
  starting transfers between devices  17.7 us (5%)
  between operations  15.7 us (5%)
    psum x3, waiting for transfers between devices, from_root(): return lax.psum(kept, axis)  104 us
    all_gather x2, waiting for transfers between devices, per_device(): picked_res = lax.all_gather(res_piece, 'cols', axis=0, tiled=True)  58.1 us
    ppermute x10, waiting for transfers between devices, gather_by_bits(): theirs = lax.ppermute(grown, axis, [(d, d ^ reach) for d in range(ways)])  54.1 us
    dot_general x8, matrix products, kernel_rows(): return jnp.dot(kernel, update, preferred_element_type=jnp.float32)  30.4 us
    ppermute x10, starting transfers between devices, gather_by_bits(): theirs = lax.ppermute(grown, axis, [(d, d ^ reach) for d in range(ways)])  17.2 us
    unnamed x19, local copies, waits for them, and re-layouts  12.9 us
    scatter-add x2, other arithmetic, per_device(): residual = residual.at[chosen_rows].add(-penalty * mine_update)  8.2 us
    scatter-add x2, other arithmetic, per_device(): coeffs = coeffs.at[chosen_rows].add(mine_update)  8.2 us
  transfers between devices with their start and end apart: 17, of which 15 were waited for; matrix products, arithmetic and copies ran while one was open for 8% of the time, Pallas kernels for 0%

profile of v1, /device:TPU:0, one launch (start us, length us, event | category | flops | bytes accessed | tf_op | source)
XLA Modules:
  0.0 346.6 jit_solution(13817953129405108673)
XLA Ops:
  14.3 3.8 %copy.18 = bf16[2048,440]{1,0:T(8,128)(2,1)} copy(bf16[2048,440]{0,1:T(8,128)(2,1)} %param.14) | data formatting | bytes 3604480 | tf_op args[0]
  18.1 3.1 gather_fusion.1
  21.2 3.2 gather_fusion.3
  25.4 26.6 %all-reduce.5.cloned.1.call-done = f32[256,147]{1,0:T(8,128)} async-done(((f32[256,147]{1,0:T(8,128)}), f32[256,147]{1,0:T(8,128)}) %all-reduce.5.cloned.1.call-update) | async-done | bytes 150544 | tf_op jit(solution)/shard_map/psum | solution.py:23
  52.1 41.4 %all-reduce.9.cloned.1.call-done = (bf16[256,440]{1,0:T(8,128)(2,1)}, bf16[256,440]{1,0:T(8,128)(2,1)}) async-done(((bf16[256,440]{1,0:T(8,128)(2,1)}, bf16[256,440]{1,0:T(8,128)(2,1)}), (bf16[256,440]{1,0:T(8,128)(2,1)}, bf16[256,440]{1,0:T(8,128)(2,1)})) %all-reduce.9.cloned.1.call-update) | async-done | bytes 450576 | tf_op jit(solution)/shard_map/psum | solution.py:23
  93.6 29.5 %all-gather.5.cloned.1.call-done = f32[2048,147]{1,0:T(8,128)} async-done(((f32[256,147]{1,0:T(8,128)}), f32[2048,147]{1,0:T(8,128)}) %all-gather.5.cloned.1.call-update) | async-done | bytes 1204240 | tf_op jit(solution)/shard_map/all_gather | solution.py:45
  123.1 2.9 fusion.18
  133.1 6.1 %collective-permute-done.2 = bf16[256,147]{1,0:T(8,128)(2,1)S(1)} collective-permute-done((bf16[256,147]{1,0:T(8,128)(2,1)S(1)}, bf16[256,147]{1,0:T(8,128)(2,1)S(1)}, u32[]{:S(2)}, u32[]{:S(2)}) %collective-permute-start.2) | collective-permute-done | bytes 75296 | tf_op jit(solution)/shard_map/ppermute | solution.py:13
  140.8 5.9 %collective-permute-done.3 = bf16[512,147]{1,0:T(8,128)(2,1)S(1)} collective-permute-done((bf16[512,147]{1,0:T(8,128)(2,1)S(1)}, bf16[512,147]{1,0:T(8,128)(2,1)S(1)}, u32[]{:S(2)}, u32[]{:S(2)}) %collective-permute-start.3) | collective-permute-done | bytes 150560 | tf_op jit(solution)/shard_map/ppermute | solution.py:13
  147.0 3.8 %collective-permute-start.4 = (bf16[1024,147]{1,0:T(8,128)(2,1)S(1)}, bf16[1024,147]{1,0:T(8,128)(2,1)S(1)}, u32[]{:S(2)}, u32[]{:S(2)}) collective-permute-start(bf16[1024,147]{1,0:T(8,128)(2,1)S(1)} %maximum_select_fusion.2), channel_id=1, source_target_pairs={{0,16},{1,17},{2,18},{3,19},{4,20},{5,21},{6,22},{7,23},{8,24},{9,... | collective-permute-start | bytes 903176 | tf_op jit(solution)/shard_map/ppermute | solution.py:13
  151.2 16.3 %collective-permute-done.4 = bf16[1024,147]{1,0:T(8,128)(2,1)S(1)} collective-permute-done((bf16[1024,147]{1,0:T(8,128)(2,1)S(1)}, bf16[1024,147]{1,0:T(8,128)(2,1)S(1)}, u32[]{:S(2)}, u32[]{:S(2)}) %collective-permute-start.4) | collective-permute-done | bytes 301088 | tf_op jit(solution)/shard_map/ppermute | solution.py:13
  171.1 14.1 %while.20 = (s32[]{:T(128)}, f32[4,512,147]{1,2,0:T(8,128)S(1)}, f32[4,512]{1,0:T(4,128)S(1)}, f32[2048]{0:T(1024)S(1)}, bf16[4,512,440]{2,1,0:T(8,128)(2,1)}, /...) while((s32[]{:T(128)}, f32[4,512,147]{1,2,0:T(8,128)S(1)}, f32[4,512]{1,0:T(4,128)S(1)}, ...), condition=%wide.region_6.9_spmd, body=%wide.region_5.8_spmd.sunk | while | flops 1236271104 | bytes 3996761 | solution.py:64
  171.2 3.5 %fusion.59 = f32[4,512,147]{1,2,0:T(8,128)S(1)} fusion(f32[4,512,147]{1,2,0:T(8,128)S(1)} %get-tuple-element.217, s32[]{:T(128)} %get-tuple-element.216, bf16[2048,147]{1,0:T(8,128)(2,1)} %get-tuple-element.230, bf16[2048,440]{1,0:T(8,128)(2,1)S(1)} %get-tuple-element.229, f32[2048]{0:T(1024)S(1)} %get-tuple-element.227, f32[512]{0:T(512)S(1)} %bitcast.70, ...), kind=kOutput, calls=%fused_computation.10.clone.1 | convolution fusion | flops 1236271104 | bytes 3992576 | tf_op jit(solution)/shard_map/while/body/eval_jaxpr/dot_general | solution.py:62
  174.7 3.5 %fusion.59 = f32[4,512,147]{1,2,0:T(8,128)S(1)} fusion(f32[4,512,147]{1,2,0:T(8,128)S(1)} %get-tuple-element.217, s32[]{:T(128)} %get-tuple-element.216, bf16[2048,147]{1,0:T(8,128)(2,1)} %get-tuple-element.230, bf16[2048,440]{1,0:T(8,128)(2,1)S(1)} %get-tuple-element.229, f32[2048]{0:T(1024)S(1)} %get-tuple-element.227, f32[512]{0:T(512)S(1)} %bitcast.70, ...), kind=kOutput, calls=%fused_computation.10.clone.1 | convolution fusion | flops 1236271104 | bytes 3992576 | tf_op jit(solution)/shard_map/while/body/eval_jaxpr/dot_general | solution.py:62
  178.2 3.5 %fusion.59 = f32[4,512,147]{1,2,0:T(8,128)S(1)} fusion(f32[4,512,147]{1,2,0:T(8,128)S(1)} %get-tuple-element.217, s32[]{:T(128)} %get-tuple-element.216, bf16[2048,147]{1,0:T(8,128)(2,1)} %get-tuple-element.230, bf16[2048,440]{1,0:T(8,128)(2,1)S(1)} %get-tuple-element.229, f32[2048]{0:T(1024)S(1)} %get-tuple-element.227, f32[512]{0:T(512)S(1)} %bitcast.70, ...), kind=kOutput, calls=%fused_computation.10.clone.1 | convolution fusion | flops 1236271104 | bytes 3992576 | tf_op jit(solution)/shard_map/while/body/eval_jaxpr/dot_general | solution.py:62
  181.7 3.5 %fusion.59 = f32[4,512,147]{1,2,0:T(8,128)S(1)} fusion(f32[4,512,147]{1,2,0:T(8,128)S(1)} %get-tuple-element.217, s32[]{:T(128)} %get-tuple-element.216, bf16[2048,147]{1,0:T(8,128)(2,1)} %get-tuple-element.230, bf16[2048,440]{1,0:T(8,128)(2,1)S(1)} %get-tuple-element.229, f32[2048]{0:T(1024)S(1)} %get-tuple-element.227, f32[512]{0:T(512)S(1)} %bitcast.70, ...), kind=kOutput, calls=%fused_computation.10.clone.1 | convolution fusion | flops 1236271104 | bytes 3992576 | tf_op jit(solution)/shard_map/while/body/eval_jaxpr/dot_general | solution.py:62
  189.5 3.1 scatter_custom_fusion.1
  194.5 36.2 %all-reduce.7.cloned.1.call-done = f32[256,147]{1,0:T(8,128)} async-done(((f32[256,147]{1,0:T(8,128)}), f32[256,147]{1,0:T(8,128)}) %all-reduce.7.cloned.1.call-update) | async-done | bytes 150544 | tf_op jit(solution)/shard_map/psum | solution.py:23
  231.5 28.6 %all-gather.9.cloned.1.call-done = f32[2048,147]{1,0:T(8,128)} async-done(((f32[256,147]{1,0:T(8,128)}), f32[2048,147]{1,0:T(8,128)}) %all-gather.9.cloned.1.call-update) | async-done | bytes 1204240 | tf_op jit(solution)/shard_map/all_gather | solution.py:45
  270.2 6.2 %collective-permute-done.7 = bf16[256,147]{1,0:T(8,128)(2,1)S(1)} collective-permute-done((bf16[256,147]{1,0:T(8,128)(2,1)S(1)}, bf16[256,147]{1,0:T(8,128)(2,1)S(1)}, u32[]{:S(2)}, u32[]{:S(2)}) %collective-permute-start.7) | collective-permute-done | bytes 75296 | tf_op jit(solution)/shard_map/ppermute | solution.py:13
  278.0 6.4 %collective-permute-done.8 = bf16[512,147]{1,0:T(8,128)(2,1)S(1)} collective-permute-done((bf16[512,147]{1,0:T(8,128)(2,1)S(1)}, bf16[512,147]{1,0:T(8,128)(2,1)S(1)}, u32[]{:S(2)}, u32[]{:S(2)}) %collective-permute-start.8) | collective-permute-done | bytes 150560 | tf_op jit(solution)/shard_map/ppermute | solution.py:13
  284.6 3.8 %collective-permute-start.9 = (bf16[1024,147]{1,0:T(8,128)(2,1)S(1)}, bf16[1024,147]{1,0:T(8,128)(2,1)S(1)}, u32[]{:S(2)}, u32[]{:S(2)}) collective-permute-start(bf16[1024,147]{1,0:T(8,128)(2,1)S(1)} %maximum_select_fusion.3), channel_id=1, source_target_pairs={{0,16},{1,17},{2,18},{3,19},{4,20},{5,21},{6,22},{7,23},{8,24},{9,... | collective-permute-start | bytes 903176 | tf_op jit(solution)/shard_map/ppermute | solution.py:13
  291.1 5.1 %scatter_custom_fusion = f32[2048,147]{1,0:T(8,128)} fusion(f32[2048,147]{1,0:T(8,128)} %copy.17, s32[256]{0:T(256)S(1)} %bitcast.79, f32[]{:T(128)S(6)} %select_n.148, bf16[2048,147]{1,0:T(8,128)(2,1)} %get-tuple-element.273, s32[]{:T(128)S(6)} %select_n.147, s32[]{:T(128)} %constant.31.clone.1), kind=kCustom, calls=%fused_computation.56 | custom fusion | flops 112896 | bytes 1335816 | tf_op jit(solution)/shard_map/scatter-add | solution.py:72
  298.3 5.8 %collective-permute-done.9 = bf16[1024,147]{1,0:T(8,128)(2,1)S(1)} collective-permute-done((bf16[1024,147]{1,0:T(8,128)(2,1)S(1)}, bf16[1024,147]{1,0:T(8,128)(2,1)S(1)}, u32[]{:S(2)}, u32[]{:S(2)}) %collective-permute-start.9) | collective-permute-done | bytes 301088 | tf_op jit(solution)/shard_map/ppermute | solution.py:13
  305.5 16.6 %while.21 = (s32[]{:T(128)}, f32[4,512,147]{1,2,0:T(8,128)S(1)}, f32[4,512]{1,0:T(4,128)S(1)}, f32[2048]{0:T(1024)S(1)}, bf16[4,512,440]{2,1,0:T(8,128)(2,1)}, /...) while((s32[]{:T(128)}, f32[4,512,147]{1,2,0:T(8,128)S(1)}, f32[4,512]{1,0:T(4,128)S(1)}, ...), condition=%wide.region_13.16_spmd, body=%wide.region_12.15_spmd.sunk | while | flops 1236271104 | bytes 3996761 | solution.py:64
  305.5 4.1 %fusion.63 = f32[4,512,147]{1,2,0:T(8,128)S(1)} fusion(f32[4,512,147]{1,2,0:T(8,128)S(1)} %get-tuple-element.241, s32[]{:T(128)} %get-tuple-element.240, bf16[2048,147]{1,0:T(8,128)(2,1)} %get-tuple-element.254, bf16[2048,440]{1,0:T(8,128)(2,1)} %get-tuple-element.253, f32[2048]{0:T(1024)S(1)} %get-tuple-element.251, f32[512]{0:T(512)S(1)} %bitcast.71, ...), kind=kOutput, calls=%fused_computation.19.clone.1 | convolution fusion | flops 1236271104 | bytes 3992576 | tf_op jit(solution)/shard_map/while/body/eval_jaxpr/dot_general | solution.py:62
  309.7 4.1 %fusion.63 = f32[4,512,147]{1,2,0:T(8,128)S(1)} fusion(f32[4,512,147]{1,2,0:T(8,128)S(1)} %get-tuple-element.241, s32[]{:T(128)} %get-tuple-element.240, bf16[2048,147]{1,0:T(8,128)(2,1)} %get-tuple-element.254, bf16[2048,440]{1,0:T(8,128)(2,1)} %get-tuple-element.253, f32[2048]{0:T(1024)S(1)} %get-tuple-element.251, f32[512]{0:T(512)S(1)} %bitcast.71, ...), kind=kOutput, calls=%fused_computation.19.clone.1 | convolution fusion | flops 1236271104 | bytes 3992576 | tf_op jit(solution)/shard_map/while/body/eval_jaxpr/dot_general | solution.py:62
  313.8 4.1 %fusion.63 = f32[4,512,147]{1,2,0:T(8,128)S(1)} fusion(f32[4,512,147]{1,2,0:T(8,128)S(1)} %get-tuple-element.241, s32[]{:T(128)} %get-tuple-element.240, bf16[2048,147]{1,0:T(8,128)(2,1)} %get-tuple-element.254, bf16[2048,440]{1,0:T(8,128)(2,1)} %get-tuple-element.253, f32[2048]{0:T(1024)S(1)} %get-tuple-element.251, f32[512]{0:T(512)S(1)} %bitcast.71, ...), kind=kOutput, calls=%fused_computation.19.clone.1 | convolution fusion | flops 1236271104 | bytes 3992576 | tf_op jit(solution)/shard_map/while/body/eval_jaxpr/dot_general | solution.py:62
  318.0 4.1 %fusion.63 = f32[4,512,147]{1,2,0:T(8,128)S(1)} fusion(f32[4,512,147]{1,2,0:T(8,128)S(1)} %get-tuple-element.241, s32[]{:T(128)} %get-tuple-element.240, bf16[2048,147]{1,0:T(8,128)(2,1)} %get-tuple-element.254, bf16[2048,440]{1,0:T(8,128)(2,1)} %get-tuple-element.253, f32[2048]{0:T(1024)S(1)} %get-tuple-element.251, f32[512]{0:T(512)S(1)} %bitcast.71, ...), kind=kOutput, calls=%fused_computation.19.clone.1 | convolution fusion | flops 1236271104 | bytes 3992576 | tf_op jit(solution)/shard_map/while/body/eval_jaxpr/dot_general | solution.py:62
  323.9 3.2 bitcast_subtract_fusion
  327.1 5.1 %scatter_custom_fusion.3 = f32[2048,147]{1,0:T(8,128)} fusion(f32[2048,147]{1,0:T(8,128)} %bitcast_subtract_fusion, s32[256]{0:T(256)S(1)} %bitcast.76, f32[]{:T(128)S(6)} %select_n.159, f32[]{:T(128)} %constant.82.clone.1, bf16[2048,147]{1,0:T(8,128)(2,1)} %get-tuple-element.274, s32[]{:T(128)S(6)} %select_n.147, s32[]{:T(128)} %constant.31.clone.1), kind=kCustom, calls=%fused_computation.49 | custom fusion | flops 150528 | bytes 1336328 | tf_op jit(solution)/shard_map/scatter-add | solution.py:71
  335.0 3.1 scatter_custom_fusion.2
  (88 shorter events, 51.3 us)
Async XLA Ops:
  7.2 44.9 %all-reduce.5.cloned.1.call-start = ((), (), s32[]{:S(2)}) async-start(), calls=%async_computation | async-start | bytes 524288 | tf_op jit(solution)/shard_map/psum | solution.py:23
  11.1 7.0 %copy-start = (f32[2048,147]{1,0:T(8,128)}, f32[2048,147]{1,0:T(8,128)S(1)}, u32[]{:S(2)}) copy-start(f32[2048,147]{1,0:T(8,128)S(1)} %copy.16) | copy-start | bytes 3612676
  13.6 80.0 %all-reduce.9.cloned.1.call-start = ((), (), s32[]{:S(2)}) async-start(), calls=%async_computation.6 | async-start | bytes 1048576 | tf_op jit(solution)/shard_map/psum | solution.py:23
  21.2 101.9 %copy-start.4 = (f32[2,64,2048]{2,1,0:T(8,128)S(1)}, f32[2,64,2048]{2,1,0:T(8,128)}, u32[]{:S(2)}) copy-start(f32[2,64,2048]{2,1,0:T(8,128)} %param.17) | copy-start | bytes 3145732
  25.4 97.7 %all-gather.5.cloned.1.call-start = ((), (), s32[]{:S(2)}) async-start(), calls=%async_computation.1 | async-start | bytes 2359296 | tf_op jit(solution)/shard_map/all_gather | solution.py:45
  52.1 116.7 %all-gather.7.cloned.1.call-start = ((), (), s32[]{:S(2)}) async-start(), calls=%async_computation.2 | async-start | bytes 2359296 | tf_op jit(solution)/shard_map/all_gather | solution.py:43
  93.6 57.2 %copy-start.2 = (bf16[2048,440]{0,1:T(8,128)(2,1)S(1)}, bf16[2048,440]{0,1:T(8,128)(2,1)}, u32[]{:S(2)}) copy-start(bf16[2048,440]{0,1:T(8,128)(2,1)} %param.14) | copy-start | bytes 5406724
  93.6 137.1 %all-reduce.7.cloned.1.call-start = ((), (), s32[]{:S(2)}) async-start(), calls=%async_computation.3 | async-start | bytes 524288 | tf_op jit(solution)/shard_map/psum | solution.py:23
  126.0 25.2 %copy-start.6 = (s32[2,256]{1,0:T(2,128)S(1)}, s32[2,256]{1,0:T(2,128)}, u32[]{:S(2)}) copy-start(s32[2,256]{1,0:T(2,128)} %param.18) | copy-start | bytes 6148
  126.0 1.3 collective-permute-start
  127.3 4.3 %collective-permute-start.1 = (bf16[128,147]{1,0:T(8,128)(2,1)S(1)}, bf16[128,147]{1,0:T(8,128)(2,1)S(1)}, u32[]{:S(2)}, u32[]{:S(2)}) collective-permute-start(bf16[128,147]{1,0:T(8,128)(2,1)S(1)} %maximum_select_fusion.8), channel_id=1, source_target_pairs={{0,2},{1,3},{2,0},{3,1},{4,6},{5,7},{6,4},{7,5},{8,10},{9,11},{10,... | collective-permute-start | bytes 112904 | tf_op jit(solution)/shard_map/ppermute | solution.py:13
  131.7 7.5 %collective-permute-start.2 = (bf16[256,147]{1,0:T(8,128)(2,1)S(1)}, bf16[256,147]{1,0:T(8,128)(2,1)S(1)}, u32[]{:S(2)}, u32[]{:S(2)}) collective-permute-start(bf16[256,147]{1,0:T(8,128)(2,1)S(1)} %maximum_select_fusion.6), channel_id=1, source_target_pairs={{0,4},{1,5},{2,6},{3,7},{4,0},{5,1},{6,2},{7,3},{8,12},{9,13},{10,... | collective-permute-start | bytes 225800 | tf_op jit(solution)/shard_map/ppermute | solution.py:13
  139.3 7.5 %collective-permute-start.3 = (bf16[512,147]{1,0:T(8,128)(2,1)S(1)}, bf16[512,147]{1,0:T(8,128)(2,1)S(1)}, u32[]{:S(2)}, u32[]{:S(2)}) collective-permute-start(bf16[512,147]{1,0:T(8,128)(2,1)S(1)} %maximum_select_fusion.4), channel_id=1, source_target_pairs={{0,8},{1,9},{2,10},{3,11},{4,12},{5,13},{6,14},{7,15},{8,0},{9,1},... | collective-permute-start | bytes 451592 | tf_op jit(solution)/shard_map/ppermute | solution.py:13
  147.0 20.5 %collective-permute-start.4 = (bf16[1024,147]{1,0:T(8,128)(2,1)S(1)}, bf16[1024,147]{1,0:T(8,128)(2,1)S(1)}, u32[]{:S(2)}, u32[]{:S(2)}) collective-permute-start(bf16[1024,147]{1,0:T(8,128)(2,1)S(1)} %maximum_select_fusion.2), channel_id=1, source_target_pairs={{0,16},{1,17},{2,18},{3,19},{4,20},{5,21},{6,22},{7,23},{8,24},{9,... | collective-permute-start | bytes 903176 | tf_op jit(solution)/shard_map/ppermute | solution.py:13
  168.7 2.4 copy-start.3
  192.7 67.5 %copy-start.5 = (f32[2,64,2048]{2,1,0:T(8,128)S(1)}, f32[2,64,2048]{2,1,0:T(8,128)}, u32[]{:S(2)}) copy-start(f32[2,64,2048]{2,1,0:T(8,128)} %param.17) | copy-start | bytes 3145732
  194.5 65.7 %all-gather.9.cloned.1.call-start = ((), (), s32[]{:S(2)}) async-start(), calls=%async_computation.4 | async-start | bytes 2359296 | tf_op jit(solution)/shard_map/all_gather | solution.py:45
  230.7 65.5 %all-gather.11.cloned.1.call-start = ((), (), s32[]{:S(2)}) async-start(), calls=%async_computation.5 | async-start | bytes 2359296 | tf_op jit(solution)/shard_map/all_gather | solution.py:43
  263.1 1.3 collective-permute-start.5
  264.3 4.3 %collective-permute-start.6 = (bf16[128,147]{1,0:T(8,128)(2,1)S(1)}, bf16[128,147]{1,0:T(8,128)(2,1)S(1)}, u32[]{:S(2)}, u32[]{:S(2)}) collective-permute-start(bf16[128,147]{1,0:T(8,128)(2,1)S(1)} %maximum_select_fusion.9), channel_id=1, source_target_pairs={{0,2},{1,3},{2,0},{3,1},{4,6},{5,7},{6,4},{7,5},{8,10},{9,11},{10,... | collective-permute-start | bytes 112904 | tf_op jit(solution)/shard_map/ppermute | solution.py:13
  268.7 7.6 %collective-permute-start.7 = (bf16[256,147]{1,0:T(8,128)(2,1)S(1)}, bf16[256,147]{1,0:T(8,128)(2,1)S(1)}, u32[]{:S(2)}, u32[]{:S(2)}) collective-permute-start(bf16[256,147]{1,0:T(8,128)(2,1)S(1)} %maximum_select_fusion.7), channel_id=1, source_target_pairs={{0,4},{1,5},{2,6},{3,7},{4,0},{5,1},{6,2},{7,3},{8,12},{9,13},{10,... | collective-permute-start | bytes 225800 | tf_op jit(solution)/shard_map/ppermute | solution.py:13
  276.4 7.9 %collective-permute-start.8 = (bf16[512,147]{1,0:T(8,128)(2,1)S(1)}, bf16[512,147]{1,0:T(8,128)(2,1)S(1)}, u32[]{:S(2)}, u32[]{:S(2)}) collective-permute-start(bf16[512,147]{1,0:T(8,128)(2,1)S(1)} %maximum_select_fusion.5), channel_id=1, source_target_pairs={{0,8},{1,9},{2,10},{3,11},{4,12},{5,13},{6,14},{7,15},{8,0},{9,1},... | collective-permute-start | bytes 451592 | tf_op jit(solution)/shard_map/ppermute | solution.py:13
  284.6 19.5 %collective-permute-start.9 = (bf16[1024,147]{1,0:T(8,128)(2,1)S(1)}, bf16[1024,147]{1,0:T(8,128)(2,1)S(1)}, u32[]{:S(2)}, u32[]{:S(2)}) collective-permute-start(bf16[1024,147]{1,0:T(8,128)(2,1)S(1)} %maximum_select_fusion.3), channel_id=1, source_target_pairs={{0,16},{1,17},{2,18},{3,19},{4,20},{5,21},{6,22},{7,23},{8,24},{9,... | collective-permute-start | bytes 903176 | tf_op jit(solution)/shard_map/ppermute | solution.py:13
  332.2 2.8 copy-start.1
Sparse Core Ops, SparseCore 0:
  13.7 38.3 all-reduce.4
  55.0 38.4 all-reduce.8
  95.4 27.5 all-gather.4
  124.8 29.1 all-gather.6
  194.6 36.0 all-reduce.6
  232.4 27.6 all-gather.8
  262.0 29.1 all-gather.10
